TPU v7x, 32 devices: a whole 2x2x4 slice. The times are simulated.
32 devices in a mesh: row: 4 (over z), col: 8 (over y, x, core).
Axes of the slice: x: 2, y: 2, z: 4, core: 2. Of those that a mesh axis runs over, the one named last changes fastest.
Arguments:
- coefs: float32 [2, 384, 16384], P(None, 'row', 'col'), may hold values from -600 to 600, as said below
- tilts: int32 [384, 2], replicated, may hold values from 8 to 48
- start_basis: float32 [384, 32], P('col'), may hold values from -6 to 6
Outputs:
- ccc: float32 [384, 384], P('row', 'col')
- basis: float32 [384, 32], P('col')
Inputs may be any that keep to these rules, and one draw needn't show every extreme that they name: `coefs`: real and imaginary parts are products of a particle scale, a coefficient scale and a bounded random value.
All inputs are finite; a program needn't handle non-finite values.
Results may differ from a plain program's by a relative error of at most 0.0003.
Values sent between devices are 32-bit elements; how exact they have to be, the bound alone decides.
A program may use at most 192 MiB of HBM per device.

v0:
```python
import math
import jax
import jax.numpy as jnp
from jax import lax
from jax.sharding import PartitionSpec as P

GRID = 32
ITERS = 4
EPS = 1e-06
HIGH = lax.Precision.HIGHEST


def wedge(tilt_rows, wave_index):
    wave_x = jnp.abs(wave_index // (GRID * (GRID // 2)) - GRID // 2)[None, :]
    wave_z = (wave_index % GRID - GRID // 2)[None, :]
    upward = wave_z * 16 <= tilt_rows[:, 1:2] * wave_x
    downward = -wave_z * 16 <= tilt_rows[:, 0:1] * wave_x
    return jnp.where(wave_z >= 0, upward, downward).astype(jnp.float32)


def inner(left, right):
    return lax.dot_general(
        left, right, (((1,), (1,)), ((), ())), precision=HIGH, preferred_element_type=jnp.float32
    )


def prepare(values, tilt_rows, wave_index):
    masks = wedge(tilt_rows, wave_index)
    paired = jnp.concatenate([values[0] * masks, values[1] * masks], axis=1)
    energy = masks * (values[0] * values[0] + values[1] * values[1])
    return (masks, paired, energy)


def local(coefs, tilts, start_basis):
    row_count = coefs.shape[1]
    slice_width = coefs.shape[2]
    col_count = start_basis.shape[0]
    col_size = lax.axis_size("col")
    total = col_count * col_size
    row_index = lax.axis_index("row")
    col_index = lax.axis_index("col")
    own_tilts = lax.dynamic_slice_in_dim(tilts, row_index * row_count, row_count, 0)
    wave_index = col_index * slice_width + jnp.arange(slice_width, dtype=jnp.int32)
    own_mask, own_pair, own_energy = prepare(coefs, own_tilts, wave_index)
    gathered = lax.all_gather(coefs, "row", axis=1, tiled=True)
    mask_j, pair_j, energy_j = prepare(gathered, tilts, wave_index)
    numer = inner(pair_j, own_pair)
    first = inner(mask_j, own_energy)
    second = inner(energy_j, own_mask)
    summed = lax.psum_scatter(
        jnp.concatenate([numer, first, second], axis=1), "col", scatter_dimension=0, tiled=True
    )
    numer = summed[:, :row_count]
    first = summed[:, row_count : 2 * row_count]
    second = summed[:, 2 * row_count :]
    block = (numer / jnp.sqrt(first * second + EPS)).T
    current = start_basis
    for step in range(ITERS):
        partial_value = jnp.dot(block, current, precision=HIGH, preferred_element_type=jnp.float32)
        summed_rows = lax.psum(partial_value, "col")
        local_gram = lax.dot_general(
            summed_rows,
            summed_rows,
            (((0,), (0,)), ((), ())),
            precision=HIGH,
            preferred_element_type=jnp.float32,
        )
        gram = lax.psum(local_gram, "row")
        factor = jnp.linalg.cholesky(gram)
        fresh = lax.linalg.triangular_solve(
            factor, summed_rows, left_side=False, lower=True, transpose_a=True
        )
        whole = lax.all_gather(fresh, "row", axis=0, tiled=True)
        current = lax.dynamic_slice_in_dim(whole, col_index * col_count, col_count, 0)
    return (block, current * math.sqrt(total))


def solution(mesh):
    in_specs = (P(None, "row", "col"), P(), P("col", None))
    out_specs = (P("row", "col"), P("col", None))
    return jax.shard_map(local, mesh=mesh, in_specs=in_specs, out_specs=out_specs, check_vma=False)
```

profile of v0, /device:TPU:0, one launch (start us, length us, event | category | flops | bytes accessed | tf_op | source)
XLA Modules:
  0.0 422.8 jit_solution(8679208534305008273)
XLA Ops:
  7.2 0.7 all-gather.6.cloned.1.call-update
  8.0 0.8 constant_dynamic-slice_fusion
  8.8 0.8 slice_reduce_fusion.1
  9.6 4.0 fusion.18
  13.6 0.4 bitcast_select_fusion.1
  14.0 113.6 %all-gather.6.cloned.1.call-done = f32[2,384,2048]{2,1,0:T(8,128)} async-done(((f32[2,96,2048]{2,1,0:T(8,128)}), f32[2,384,2048]{2,1,0:T(8,128)}) %all-gather.6.cloned.1.call-update) | async-done | bytes 6291472 | tf_op jit(solution)/shard_map/all_gather | solution.py:45
  127.6 4.1 fusion.10
  131.8 6.0 %fusion = f32[384,96]{0,1:T(8,128)S(1)} fusion(f32[384,2048]{1,0:T(8,128)S(1)} %get-tuple-element.13, f32[384,2048]{1,0:T(8,128)S(1)} %get-tuple-element.12, f32[96,2048]{1,0:T(8,128)S(1)} %get-tuple-element.15, f32[96,2048]{1,0:T(8,128)S(1)} %get-tuple-element.14), kind=kOutput, calls=%fused_computation | convolution fusion | flops 1813905408 | bytes 8011776 | tf_op jit(solution)/shard_map/dot_general | solution.py:22
  137.8 3.2 fusion.4
  141.1 1.2 copy.44
  142.3 32.7 %reduce-scatter.4.cloned.1.call-done = f32[48,288]{1,0:T(8,128)} async-done(((f32[384,288]{1,0:T(8,128)}), f32[48,288]{1,0:T(8,128)}) %reduce-scatter.4.cloned.1.call-update) | async-done | bytes 55312
  175.0 0.9 fusion.67
  176.5 22.5 %psum.56 = f32[96,32]{0,1:T(8,128)S(1)} all-reduce(f32[96,32]{0,1:T(8,128)S(1)} %fusion.68), channel_id=1, replica_groups=mesh['row'=4,'col'=8] {'col'}, use_global_device_ids=true, to_apply=%region_1.2 | all-reduce | flops 3072 | bytes 24576 | tf_op jit(solution)/shard_map/psum | solution.py:60
  199.2 18.7 %psum.57 = f32[32,32]{0,1:T(8,128)S(1)} all-reduce(f32[32,32]{0,1:T(8,128)S(1)} %fusion.69), channel_id=1, replica_groups=mesh['row'=4,'col'=8] {'row'}, use_global_device_ids=true, to_apply=%region_2.3 | all-reduce | flops 1024 | bytes 8192 | tf_op jit(solution)/shard_map/psum | solution.py:68
  218.0 2.9 cholesky.74
  220.9 0.6 compare_reduce_fusion.3
  221.6 0.7 fusion.24
  222.2 2.4 custom-call.8
  224.6 0.2 convolution_bitcast_fusion.3
  224.9 0.7 copy.39
  225.6 13.1 %all-gather = f32[4,96,32]{1,2,0:T(8,128)S(1)} all-gather(f32[1,96,32]{1,2,0:T(8,128)S(1)} %convolution_bitcast_fusion.3), channel_id=1, replica_groups=mesh['row'=4,'col'=8] {'row'}, dimensions={0}, use_global_device_ids=true | all-gather | bytes 61440 | tf_op jit(solution)/shard_map/all_gather | solution.py:73
  239.1 22.3 %psum.58 = f32[96,32]{0,1:T(8,128)S(1)} all-reduce(f32[96,32]{0,1:T(8,128)S(1)} %fusion.46), channel_id=1, replica_groups=mesh['row'=4,'col'=8] {'col'}, use_global_device_ids=true, to_apply=%region_5.8 | all-reduce | flops 3072 | bytes 24576 | tf_op jit(solution)/shard_map/psum | solution.py:60
  261.5 15.5 %psum.59 = f32[32,32]{0,1:T(8,128)S(1)} all-reduce(f32[32,32]{0,1:T(8,128)S(1)} %fusion.70), channel_id=1, replica_groups=mesh['row'=4,'col'=8] {'row'}, use_global_device_ids=true, to_apply=%region_6.9 | all-reduce | flops 1024 | bytes 8192 | tf_op jit(solution)/shard_map/psum | solution.py:68
  277.2 2.9 cholesky.85
  280.1 0.6 compare_reduce_fusion.2
  280.8 0.7 fusion.25
  281.4 2.4 custom-call.9
  283.8 0.2 convolution_bitcast_fusion.2
  284.1 13.1 %all-gather.1 = f32[4,96,32]{1,2,0:T(8,128)S(1)} all-gather(f32[1,96,32]{1,2,0:T(8,128)S(1)} %convolution_bitcast_fusion.2), channel_id=1, replica_groups=mesh['row'=4,'col'=8] {'row'}, dimensions={0}, use_global_device_ids=true | all-gather | bytes 61440 | tf_op jit(solution)/shard_map/all_gather | solution.py:73
  297.4 0.2 fusion.44
  297.6 22.3 %psum.60 = f32[96,32]{0,1:T(8,128)S(1)} all-reduce(f32[96,32]{0,1:T(8,128)S(1)} %fusion.44), channel_id=1, replica_groups=mesh['row'=4,'col'=8] {'col'}, use_global_device_ids=true, to_apply=%region_7.10 | all-reduce | flops 3072 | bytes 24576 | tf_op jit(solution)/shard_map/psum | solution.py:60
  320.1 16.3 %psum.61 = f32[32,32]{0,1:T(8,128)S(1)} all-reduce(f32[32,32]{0,1:T(8,128)S(1)} %fusion.71), channel_id=1, replica_groups=mesh['row'=4,'col'=8] {'row'}, use_global_device_ids=true, to_apply=%region_8.11 | all-reduce | flops 1024 | bytes 8192 | tf_op jit(solution)/shard_map/psum | solution.py:68
  336.5 2.9 cholesky.96
  339.4 0.6 compare_reduce_fusion.1
  340.1 0.7 fusion.26
  340.7 2.4 custom-call.10
  343.2 0.2 convolution_bitcast_fusion.1
  343.4 13.1 %all-gather.2 = f32[4,96,32]{1,2,0:T(8,128)S(1)} all-gather(f32[1,96,32]{1,2,0:T(8,128)S(1)} %convolution_bitcast_fusion.1), channel_id=1, replica_groups=mesh['row'=4,'col'=8] {'row'}, dimensions={0}, use_global_device_ids=true | all-gather | bytes 61440 | tf_op jit(solution)/shard_map/all_gather | solution.py:73
  356.7 0.2 fusion.42
  356.9 22.3 %psum.62 = f32[96,32]{0,1:T(8,128)S(1)} all-reduce(f32[96,32]{0,1:T(8,128)S(1)} %fusion.42), channel_id=1, replica_groups=mesh['row'=4,'col'=8] {'col'}, use_global_device_ids=true, to_apply=%region_9.12 | all-reduce | flops 3072 | bytes 24576 | tf_op jit(solution)/shard_map/psum | solution.py:60
  379.4 15.5 %psum.63 = f32[32,32]{0,1:T(8,128)S(1)} all-reduce(f32[32,32]{0,1:T(8,128)S(1)} %fusion.72), channel_id=1, replica_groups=mesh['row'=4,'col'=8] {'row'}, use_global_device_ids=true, to_apply=%region_10.13 | all-reduce | flops 1024 | bytes 8192 | tf_op jit(solution)/shard_map/psum | solution.py:68
  395.0 2.9 cholesky.107
  398.0 0.6 compare_reduce_fusion
  398.6 0.7 fusion.27
  399.3 2.4 custom-call.11
  401.7 0.2 convolution_bitcast_fusion
  402.0 13.1 %all-gather.3 = f32[4,96,32]{1,2,0:T(8,128)S(1)} all-gather(f32[1,96,32]{1,2,0:T(8,128)S(1)} %convolution_bitcast_fusion), channel_id=1, replica_groups=mesh['row'=4,'col'=8] {'row'}, dimensions={0}, use_global_device_ids=true | all-gather | bytes 61440 | tf_op jit(solution)/shard_map/all_gather | solution.py:73
  415.2 0.7 dynamic-slice_multiply_fusion
  (44 shorter events, 2.5 us)
Async XLA Ops:
  7.2 169.1 %copy-start = (f32[48,32]{0,1:T(8,128)S(1)}, f32[48,32]{0,1:T(8,128)}, u32[]{:S(2)}) copy-start(f32[48,32]{0,1:T(8,128)} %param.8) | copy-start | bytes 18436
  7.2 120.5 %all-gather.6.cloned.1.call-start = ((), (), s32[]{:S(2)}) async-start(), calls=%async_computation.1 | async-start | bytes 7864320 | tf_op jit(solution)/shard_map/all_gather | solution.py:45
  7.9 167.1 %reduce-scatter.4.cloned.1.call-start = ((), (), s32[]{:S(2)}) async-start(), calls=%async_computation.2 | async-start | bytes 663552
  9.6 4.0 copy-start.1
  131.8 6.0 %copy-start.2 = (f32[2,384,2048]{2,1,0:T(8,128)S(1)}, f32[2,384,2048]{2,1,0:T(8,128)}, u32[]{:S(2)}) copy-start(f32[2,384,2048]{2,1,0:T(8,128)} %all-gather.6.cloned.1.call-done) | copy-start | bytes 18874372
Sparse Core Ops, SparseCore 0:
  9.6 118.0 all-gather.5
  142.5 32.5 reduce-scatter.3
where the time goes:
time: 423 us
  blocking collectives  208 us (49%)
  waiting for transfers between devices  147 us (35%)
  other arithmetic  32.1 us (8%)
  matrix products  15.6 us (4%)
  between operations  14.4 us (3%)
  local copies, waits for them, and re-layouts  5.54 us (1%)
    all_gather x1, waiting for transfers between devices, local(): gathered = lax.all_gather(coefs, 'row', axis=1, tiled=True)  114 us
    psum x4, blocking collectives, local(): summed_rows = lax.psum(partial_value, 'col')  89.5 us
    psum x4, blocking collectives, local(): gram = lax.psum(local_gram, 'row')  66.1 us
    all_gather x4, blocking collectives, local(): whole = lax.all_gather(fresh, 'row', axis=0, tiled=True)  52.5 us
    unnamed x3, waiting for transfers between devices  33.4 us
    another operation x12, other arithmetic, local(): factor = jnp.linalg.cholesky(gram)  14.4 us
    dot_general x3, matrix products, inner(): lax.dot_general(left, right, (((1,), (1,)), ((), ())), precision=HIGH, pr...  13.2 us
    another operation x8, other arithmetic, local(): lax.linalg.triangular_solve(factor, summed_rows, left_side=False, lower=T...  12.3 us
  transfers between devices with their start and end apart: 2, of which 2 were waited for; matrix products, arithmetic and copies ran while one was open for 1% of the time, Pallas kernels for 0%

commit v1 on v0

--- a/solution.py
+++ b/solution.py
@@ -57,7 +57,8 @@
     current = start_basis
     for step in range(ITERS):
         partial_value = jnp.dot(block, current, precision=HIGH, preferred_element_type=jnp.float32)
-        summed_rows = lax.psum(partial_value, "col")
+        parts = lax.all_gather(partial_value, "col")
+        summed_rows = jnp.sum(parts, axis=0)
         local_gram = lax.dot_general(
             summed_rows,
             summed_rows,

time: 423 us -> 369 us (0.87)
  blocking collectives: 208 us -> 154 us
    psum x4 -> x0, blocking collectives: 89.5 us -> none  [local(): summed_rows = lax.psum(partial_value, 'col')]
    all_gather x0 -> x4, blocking collectives: none -> 34.9 us  [local(): parts = lax.all_gather(partial_value, 'col')]
  transfers between devices with their start and end apart: 2 -> 2, of which waited for: 2 -> 2; matrix products, arithmetic and copies ran while one was open for 1% -> 2% of each run, Pallas kernels for 0% -> 0%
where the time goes in v1:
time: 369 us; the launch traced here: 368 us
  blocking collectives  154 us (42%)
  waiting for transfers between devices  147 us (40%)
  other arithmetic  32.2 us (9%)
  matrix products  15.6 us (4%)
  between operations  14.4 us (4%)
  local copies, waits for them, and re-layouts  5.56 us (2%)
    all_gather x1, waiting for transfers between devices, local(): gathered = lax.all_gather(coefs, 'row', axis=1, tiled=True)  114 us
    psum x4, blocking collectives, local(): gram = lax.psum(local_gram, 'row')  66.3 us
    all_gather x4, blocking collectives, local(): whole = lax.all_gather(fresh, 'row', axis=0, tiled=True)  52.5 us
    all_gather x4, blocking collectives, local(): parts = lax.all_gather(partial_value, 'col')  34.9 us
    unnamed x3, waiting for transfers between devices  33.4 us
    another operation x12, other arithmetic, local(): factor = jnp.linalg.cholesky(gram)  14.4 us
    dot_general x3, matrix products, inner(): lax.dot_general(left, right, (((1,), (1,)), ((), ())), precision=HIGH, pr...  13.2 us
    another operation x8, other arithmetic, local(): lax.linalg.triangular_solve(factor, summed_rows, left_side=False, lower=T...  12.3 us
  transfers between devices with their start and end apart: 2, of which 2 were waited for; matrix products, arithmetic and copies ran while one was open for 2% of the time, Pallas kernels for 0%

profile of v1, /device:TPU:0, one launch (start us, length us, event | category | flops | bytes accessed | tf_op | source)
XLA Modules:
  0.0 368.4 jit_solution(15705106810537005991)
XLA Ops:
  7.2 0.7 all-gather.14.cloned.1.call-update
  8.0 0.8 constant_dynamic-slice_fusion
  8.8 0.8 slice_reduce_fusion.1
  9.6 4.0 %fusion.18 = f32[384,96]{0,1:T(8,128)S(1)} fusion(f32[2,96,2048]{2,1,0:T(8,128)} %param.6, s32[96]{0:T(128)S(1)} %get-tuple-element.20, s32[2048]{0:T(1024)S(1)} %get-tuple-element.22, s32[2048]{0:T(1024)S(1)} %get-tuple-element.21, s32[96]{0:T(128)S(1)} %get-tuple-element.19, s32[2048]{0:T(1024)S(1)} %broadcast_multiply_fusion, ...), kind=kOutput, calls=%fused_computation.32 | convolution fusion | flops 911671296 | bytes 1778688 | tf_op jit(solution)/shard_map/dot_general | solution.py:22
  13.6 0.4 bitcast_select_fusion.1
  14.0 113.6 %all-gather.14.cloned.1.call-done = f32[2,384,2048]{2,1,0:T(8,128)} async-done(((f32[2,96,2048]{2,1,0:T(8,128)}), f32[2,384,2048]{2,1,0:T(8,128)}) %all-gather.14.cloned.1.call-update) | async-done | bytes 6291472 | tf_op jit(solution)/shard_map/all_gather | solution.py:45
  127.6 4.1 %fusion.10 = (f32[384,2048]{1,0:T(8,128)S(1)}, f32[384,2048]{1,0:T(8,128)S(1)}) fusion(f32[2,384,2048]{2,1,0:T(8,128)} %all-gather.14.cloned.1.call-done, s32[384]{0:T(512)S(1)} %get-tuple-element.11, s32[2048]{0:T(1024)S(1)} %get-tuple-element.22, s32[2048]{0:T(1024)S(1)} %get-tuple-element.21, s32[384]{0:T(512)S(1)} %get-tuple-element.10, ...), kind=kLoop, calls=%fused_computation.14 | loop fusion | flops 5505024 | bytes 12612608 | tf_op jit(solution)/shard_map/mul | solution.py:29
  131.8 6.0 %fusion = f32[384,96]{0,1:T(8,128)S(1)} fusion(f32[384,2048]{1,0:T(8,128)S(1)} %get-tuple-element.13, f32[384,2048]{1,0:T(8,128)S(1)} %get-tuple-element.12, f32[96,2048]{1,0:T(8,128)S(1)} %get-tuple-element.15, f32[96,2048]{1,0:T(8,128)S(1)} %get-tuple-element.14), kind=kOutput, calls=%fused_computation | convolution fusion | flops 1813905408 | bytes 8011776 | tf_op jit(solution)/shard_map/dot_general | solution.py:22
  137.8 3.2 fusion.4
  141.1 1.2 copy.44
  142.3 32.7 %reduce-scatter.4.cloned.1.call-done = f32[48,288]{1,0:T(8,128)} async-done(((f32[384,288]{1,0:T(8,128)}), f32[48,288]{1,0:T(8,128)}) %reduce-scatter.4.cloned.1.call-update) | async-done | bytes 55312
  175.0 0.9 fusion.64
  176.5 0.7 copy.39
  177.2 9.1 %all-gather.4 = f32[8,96,32]{1,2,0:T(8,128)S(1)} all-gather(f32[1,96,32]{1,2,0:T(8,128)S(1)} %convolution_bitcast_fusion.7), channel_id=2, replica_groups=mesh['row'=4,'col'=8] {'col'}, dimensions={0}, use_global_device_ids=true | all-gather | bytes 110592 | tf_op jit(solution)/shard_map/all_gather | solution.py:60
  186.5 18.7 %psum.28 = f32[32,32]{0,1:T(8,128)S(1)} all-reduce(f32[32,32]{0,1:T(8,128)S(1)} %fusion.65), channel_id=1, replica_groups=mesh['row'=4,'col'=8] {'row'}, use_global_device_ids=true, to_apply=%region_2.3 | all-reduce | flops 1024 | bytes 8192 | tf_op jit(solution)/shard_map/psum | solution.py:69
  205.3 2.9 cholesky.74
  208.2 0.6 compare_reduce_fusion.3
  208.9 0.7 fusion.24
  209.6 2.4 custom-call.8
  212.0 0.2 convolution_bitcast_fusion.6
  212.2 13.1 %all-gather.5 = f32[4,96,32]{1,2,0:T(8,128)S(1)} all-gather(f32[1,96,32]{1,2,0:T(8,128)S(1)} %convolution_bitcast_fusion.6), channel_id=1, replica_groups=mesh['row'=4,'col'=8] {'row'}, dimensions={0}, use_global_device_ids=true | all-gather | bytes 61440 | tf_op jit(solution)/shard_map/all_gather | solution.py:74
  225.5 0.2 convolution_bitcast_fusion.5
  225.7 8.3 %all-gather.6 = f32[8,96,32]{1,2,0:T(8,128)S(1)} all-gather(f32[1,96,32]{1,2,0:T(8,128)S(1)} %convolution_bitcast_fusion.5), channel_id=3, replica_groups=mesh['row'=4,'col'=8] {'col'}, dimensions={0}, use_global_device_ids=true | all-gather | bytes 110592 | tf_op jit(solution)/shard_map/all_gather | solution.py:60
  234.2 15.5 %psum.29 = f32[32,32]{0,1:T(8,128)S(1)} all-reduce(f32[32,32]{0,1:T(8,128)S(1)} %fusion.66), channel_id=1, replica_groups=mesh['row'=4,'col'=8] {'row'}, use_global_device_ids=true, to_apply=%region_6.9 | all-reduce | flops 1024 | bytes 8192 | tf_op jit(solution)/shard_map/psum | solution.py:69
  249.8 2.9 cholesky.85
  252.7 0.6 compare_reduce_fusion.2
  253.4 0.7 fusion.25
  254.1 2.4 custom-call.9
  256.5 0.2 convolution_bitcast_fusion.4
  256.7 13.1 %all-gather.7 = f32[4,96,32]{1,2,0:T(8,128)S(1)} all-gather(f32[1,96,32]{1,2,0:T(8,128)S(1)} %convolution_bitcast_fusion.4), channel_id=1, replica_groups=mesh['row'=4,'col'=8] {'row'}, dimensions={0}, use_global_device_ids=true | all-gather | bytes 61440 | tf_op jit(solution)/shard_map/all_gather | solution.py:74
  270.0 0.2 convolution_bitcast_fusion.3
  270.2 9.2 %all-gather.8 = f32[8,96,32]{1,2,0:T(8,128)S(1)} all-gather(f32[1,96,32]{1,2,0:T(8,128)S(1)} %convolution_bitcast_fusion.3), channel_id=4, replica_groups=mesh['row'=4,'col'=8] {'col'}, dimensions={0}, use_global_device_ids=true | all-gather | bytes 110592 | tf_op jit(solution)/shard_map/all_gather | solution.py:60
  279.6 16.3 %psum.30 = f32[32,32]{0,1:T(8,128)S(1)} all-reduce(f32[32,32]{0,1:T(8,128)S(1)} %fusion.67), channel_id=1, replica_groups=mesh['row'=4,'col'=8] {'row'}, use_global_device_ids=true, to_apply=%region_8.11 | all-reduce | flops 1024 | bytes 8192 | tf_op jit(solution)/shard_map/psum | solution.py:69
  296.0 2.9 cholesky.96
  298.9 0.6 compare_reduce_fusion.1
  299.6 0.7 fusion.26
  300.2 2.4 custom-call.10
  302.7 0.2 convolution_bitcast_fusion.2
  302.9 13.1 %all-gather.9 = f32[4,96,32]{1,2,0:T(8,128)S(1)} all-gather(f32[1,96,32]{1,2,0:T(8,128)S(1)} %convolution_bitcast_fusion.2), channel_id=1, replica_groups=mesh['row'=4,'col'=8] {'row'}, dimensions={0}, use_global_device_ids=true | all-gather | bytes 61440 | tf_op jit(solution)/shard_map/all_gather | solution.py:74
  316.4 8.3 %all-gather.10 = f32[8,96,32]{1,2,0:T(8,128)S(1)} all-gather(f32[1,96,32]{1,2,0:T(8,128)S(1)} %convolution_bitcast_fusion.1), channel_id=5, replica_groups=mesh['row'=4,'col'=8] {'col'}, dimensions={0}, use_global_device_ids=true | all-gather | bytes 110592 | tf_op jit(solution)/shard_map/all_gather | solution.py:60
  324.9 15.7 %psum.31 = f32[32,32]{0,1:T(8,128)S(1)} all-reduce(f32[32,32]{0,1:T(8,128)S(1)} %fusion.68), channel_id=1, replica_groups=mesh['row'=4,'col'=8] {'row'}, use_global_device_ids=true, to_apply=%region_10.13 | all-reduce | flops 1024 | bytes 8192 | tf_op jit(solution)/shard_map/psum | solution.py:69
  340.6 2.9 cholesky.107
  343.6 0.6 compare_reduce_fusion
  344.2 0.7 fusion.27
  344.9 2.4 custom-call.11
  347.3 0.2 convolution_bitcast_fusion
  347.6 13.1 %all-gather.11 = f32[4,96,32]{1,2,0:T(8,128)S(1)} all-gather(f32[1,96,32]{1,2,0:T(8,128)S(1)} %convolution_bitcast_fusion), channel_id=1, replica_groups=mesh['row'=4,'col'=8] {'row'}, dimensions={0}, use_global_device_ids=true | all-gather | bytes 61440 | tf_op jit(solution)/shard_map/all_gather | solution.py:74
  360.8 0.7 dynamic-slice_multiply_fusion
  (48 shorter events, 2.5 us)
Async XLA Ops:
  7.2 169.1 %copy-start = (f32[48,32]{0,1:T(8,128)S(1)}, f32[48,32]{0,1:T(8,128)}, u32[]{:S(2)}) copy-start(f32[48,32]{0,1:T(8,128)} %param.8) | copy-start | bytes 18436
  7.2 120.5 %all-gather.14.cloned.1.call-start = ((), (), s32[]{:S(2)}) async-start(), calls=%async_computation.1 | async-start | bytes 7864320 | tf_op jit(solution)/shard_map/all_gather | solution.py:45
  7.9 167.1 %reduce-scatter.4.cloned.1.call-start = ((), (), s32[]{:S(2)}) async-start(), calls=%async_computation.2 | async-start | bytes 663552
  9.6 4.0 %copy-start.1 = (f32[2,96,2048]{2,1,0:T(8,128)S(1)}, f32[2,96,2048]{2,1,0:T(8,128)}, u32[]{:S(2)}) copy-start(f32[2,96,2048]{2,1,0:T(8,128)} %param.6) | copy-start | bytes 4718596
  131.8 6.0 %copy-start.2 = (f32[2,384,2048]{2,1,0:T(8,128)S(1)}, f32[2,384,2048]{2,1,0:T(8,128)}, u32[]{:S(2)}) copy-start(f32[2,384,2048]{2,1,0:T(8,128)} %all-gather.14.cloned.1.call-done) | copy-start | bytes 18874372
Sparse Core Ops, SparseCore 0:
  9.6 118.0 all-gather.13
  142.5 32.5 reduce-scatter.3
